TPU v7x, 32 devices: a whole 2x2x4 slice. The times are simulated.
32 devices in a mesh: clip: 2 (over x), seq: 16 (over z, y, core).
Axes of the slice: x: 2, y: 2, z: 4, core: 2. Of those that a mesh axis runs over, the one named last changes fastest.
Arguments:
- hidden: bfloat16 [2, 1792, 1536], P(None, ('clip', 'seq')), parts along dimension 1, may hold values from -6 to 6
- latent: float32 [1792, 100], P(('clip', 'seq')), parts along dimension 0, may hold values from -6 to 6
- lengths: int32 [2], P('clip'), parts along dimension 0, may hold values from 448 to 896
- step_index: int32 [1], replicated, may hold values from 0 to 31
- guidance: float32 [1], replicated, may hold values from 1.5 to 2.5
- modulation: float32 [5, 1536], replicated, may hold values from -2.5 to 2.5
- conv_kernel: float32 [31, 1536], replicated, may hold values from -1 to 1
- w_qkv: bfloat16 [1536, 3072], replicated, may hold values from -1 to 1
- w_out: bfloat16 [1024, 1536], replicated, may hold values from -0.1875 to 0.1875
- w_mel: bfloat16 [1536, 100], replicated, may hold values from -0.15625 to 0.15625
Outputs:
- velocity: float32 [1792, 100], P(('clip', 'seq')), parts along dimension 0
- estimate: float32 [1792, 100], P(('clip', 'seq')), parts along dimension 0
There are 2 independent parts, one for each index of `clip`. A program takes and returns all parts, laid end to end along the dimension named above; an argument that names none is the same for every part. Nothing has to cross between parts.
All inputs are finite; a program needn't handle non-finite values.
Results may differ from a plain program's by a relative error of at most 0.0061.
Values may be sent and summed in bfloat16 or wider, within the bound.
A program may use at most 192 MiB of HBM per device.

v0:
```python
import functools

import jax
import jax.numpy as jnp
import numpy as np
from jax import lax
from jax.experimental import pallas as pl
from jax.experimental.pallas import tpu as pltpu
from jax.sharding import PartitionSpec as P

HEADS = 16
HEAD_DIM = 64
STEPS = 32
LANES = 128
EPSILON = 1e-06
NEGATIVE = -1e30
MESH = pl.DeviceIdType.MESH
ROW_BLOCK = 16
GROUPS = 4
BLOCKS = 2


def layer_norm(values, shift_row, scale_row):
    mean_value = jnp.mean(values, axis=-1, keepdims=True)
    centered = values - mean_value
    variance = jnp.mean(centered * centered, axis=-1, keepdims=True)
    return centered * lax.rsqrt(variance + EPSILON) * (1.0 + scale_row) + shift_row


def mish(values):
    grown = jnp.exp(jnp.minimum(values, 30.0))
    top = grown * (grown + 2.0)
    return values * (top / (top + 2.0))


def kernel(
    count,
    subs,
    frame_rows,
    taps,
    length_ref,
    guidance_ref,
    hidden_hbm,
    modulation_hbm,
    conv_hbm,
    qkv_hbm,
    out_hbm,
    mel_hbm,
    row_table_hbm,
    base_table_hbm,
    guided_ref,
    hid,
    halo,
    modulation,
    conv,
    w_qkv,
    w_out,
    w_mel,
    row_table,
    base_table,
    tables,
    residual,
    normed,
    q_send,
    kv_send,
    q_recv,
    kv_recv,
    o_send,
    o_recv,
    attended,
    bias,
    local_sem,
    qkv_sem,
    halo_send_sem,
    halo_recv_sem,
    q_send_sem,
    q_recv_sem,
    kv_send_sem,
    kv_recv_sem,
    o_send_sem,
    o_recv_sem,
):
    copies = hid.shape[0]
    padded = hid.shape[1]
    reach = halo.shape[2]
    width = hid.shape[2]
    units = q_send.shape[0]
    per_group = units // GROUPS
    attention_width = w_out.shape[0]
    me = lax.axis_index("seq")
    length = length_ref[0]
    own_rows = pl.ds(0, frame_rows)

    pulls = [
        (hidden_hbm, hid.at[:, pl.ds(0, frame_rows), :]),
        (conv_hbm, conv),
        (modulation_hbm, modulation),
        (row_table_hbm, row_table),
        (base_table_hbm.at[me], base_table),
    ]
    local = [
        pltpu.make_async_copy(source, target, local_sem.at[i])
        for i, (source, target) in enumerate(pulls)
    ]
    for copy in local:
        copy.start()
    chunks = qkv_sem.shape[0]
    depth = width // chunks
    weights = [
        pltpu.make_async_copy(
            qkv_hbm.at[pl.ds(i * depth, depth)], w_qkv.at[pl.ds(i * depth, depth)], qkv_sem.at[i]
        )
        for i in range(chunks)
    ]
    for copy in weights:
        copy.start()
    late = [
        pltpu.make_async_copy(out_hbm, w_out, local_sem.at[len(pulls)]),
        pltpu.make_async_copy(mel_hbm, w_mel, local_sem.at[len(pulls) + 1]),
    ]
    for copy in late:
        copy.start()

    barrier = pltpu.get_barrier_semaphore()

    def greet(step, carry):
        pl.semaphore_signal(
            barrier, inc=1, device_id={"seq": (me + step) % count}, device_id_type=MESH
        )
        return carry

    lax.fori_loop(1, count, greet, 0)
    hid[:, pl.ds(frame_rows, padded - frame_rows), :] = jnp.zeros(
        (copies, padded - frame_rows, width), hid.dtype
    )
    spare = pl.ds(frame_rows, padded - frame_rows)
    for buffer in (q_recv, o_recv):
        buffer[:, spare, :] = jnp.zeros((units, padded - frame_rows, LANES), buffer.dtype)
    kv_recv[:, :, spare, :] = jnp.zeros((count, 2, padded - frame_rows, LANES), kv_recv.dtype)
    pl.semaphore_wait(barrier, count - 1)

    local[0].wait()
    to_right = pltpu.make_async_remote_copy(
        src_ref=hid.at[:, pl.ds(frame_rows - reach, reach), :],
        dst_ref=halo.at[0],
        send_sem=halo_send_sem.at[0],
        recv_sem=halo_recv_sem.at[0],
        device_id={"seq": (me + 1) % count},
        device_id_type=MESH,
    )
    to_left = pltpu.make_async_remote_copy(
        src_ref=hid.at[:, pl.ds(0, reach), :],
        dst_ref=halo.at[1],
        send_sem=halo_send_sem.at[1],
        recv_sem=halo_recv_sem.at[1],
        device_id={"seq": (me + count - 1) % count},
        device_id_type=MESH,
    )

    @pl.when(me < count - 1)
    def _():
        to_right.start()

    @pl.when(me > 0)
    def _():
        to_left.start()

    @pl.when(me == 0)
    def _():
        halo[0] = jnp.zeros(halo.shape[1:], halo.dtype)

    @pl.when(me == count - 1)
    def _():
        halo[1] = jnp.zeros(halo.shape[1:], halo.dtype)

    for copy in local[1:]:
        copy.wait()

    base_cos = base_table[0:1, :]
    base_sin = base_table[1:2, :]
    row_cos = row_table[0]
    row_sin = row_table[1]
    lane = lax.broadcasted_iota(jnp.int32, (padded, LANES), 1)
    lower = lane % HEAD_DIM < HEAD_DIM // 2
    cosine = row_cos * base_cos - row_sin * base_sin
    sine = row_sin * base_cos + row_cos * base_sin
    sine = jnp.where(lower, -sine, sine)
    for c in range(copies):
        tables[0, pl.ds(c * padded, padded), :] = cosine
        tables[1, pl.ds(c * padded, padded), :] = sine
    key_index = lax.broadcasted_iota(jnp.int32, bias.shape, 1)
    key_row = key_index % padded
    key_position = (key_index // padded) * frame_rows + key_row
    key_live = (key_row < frame_rows) & (key_position < length)
    bias[...] = jnp.where(key_live, 0.0, NEGATIVE)

    @pl.when(me < count - 1)
    def _():
        to_right.wait_send()
        to_left.wait_recv()

    @pl.when(me > 0)
    def _():
        to_left.wait_send()
        to_right.wait_recv()

    window = frame_rows + 2 * reach
    position = (
        me * frame_rows - reach + lax.broadcasted_iota(jnp.int32, (window, LANES), 0)
    )
    is_live = (position >= 0) & (position < length)
    lead = reach - taps // 2

    def convolve(block, carry):
        columns = pl.ds(pl.multiple_of(block * LANES, LANES), LANES)
        for c in range(copies):
            own = hid[c, :, columns].astype(jnp.float32)
            cells = jnp.concatenate(
                [
                    halo[0, c, :, columns].astype(jnp.float32),
                    own[:frame_rows],
                    halo[1, c, :, columns].astype(jnp.float32),
                ],
                axis=0,
            )
            cells = jnp.where(is_live, cells, 0.0)
            total = jnp.zeros((padded, LANES), jnp.float32)
            for shift in range(8):
                part = None
                for first in range(0, reach * 2, 8):
                    tap = first + shift - lead
                    if 0 <= tap < taps:
                        term = cells[first : first + padded] * conv[pl.ds(tap, 1), columns]
                        part = term if part is None else part + term
                if part is not None:
                    total = total + (pltpu.roll(part, padded - shift, 0) if shift else part)
            residual[pl.ds(c * padded, padded), columns] = own + mish(total)
        return carry

    lax.fori_loop(0, width // LANES, convolve, 0)

    def normalise(first):
        def one(block, carry):
            rows = pl.ds(pl.multiple_of(block * ROW_BLOCK, ROW_BLOCK), ROW_BLOCK)
            normed[rows, :] = layer_norm(
                residual[rows, :], modulation[first : first + 1, :], modulation[first + 1 : first + 2, :]
            ).astype(normed.dtype)
            return carry

        lax.fori_loop(0, copies * padded // ROW_BLOCK, one, 0)

    normalise(0)
    for copy in weights:
        copy.wait()

    my_group = me * GROUPS // count
    my_high = my_group // 2
    my_low = my_group % 2

    def group_at(step):
        return ((my_high + (3 - step) // 2) % 2) * 2 + (my_low + (step + 1) // 2) % 2

    my_unit = me // subs
    my_sub = me % subs
    query_sub = me // units
    query_slot = me % units

    def query_copy(unit):
        return pltpu.make_async_remote_copy(
            src_ref=q_send.at[unit, own_rows],
            dst_ref=q_recv.at[query_slot, own_rows],
            send_sem=q_send_sem.at[unit],
            recv_sem=q_recv_sem.at[query_slot],
            device_id={"seq": unit * subs + query_sub},
            device_id_type=MESH,
        )

    def key_value_copy(unit, sub):
        return pltpu.make_async_remote_copy(
            src_ref=kv_send.at[unit, :, own_rows],
            dst_ref=kv_recv.at[me, :, own_rows],
            send_sem=kv_send_sem.at[unit * subs + sub],
            recv_sem=kv_recv_sem.at[me],
            device_id={"seq": unit * subs + sub},
            device_id_type=MESH,
        )

    pair_width = 2 * LANES
    tile_lower = lax.broadcasted_iota(jnp.int32, (copies * padded, LANES), 1) % HEAD_DIM < (
        HEAD_DIM // 2
    )

    def rotate(tile, factor):
        half = HEAD_DIM // 2
        other = jnp.where(
            tile_lower, pltpu.roll(tile, LANES - half, 1), pltpu.roll(tile, half, 1)
        )
        return (tile * tables[0] + other * tables[1]) * factor

    def product(part, group):
        start = pl.multiple_of(part * attention_width + group * pair_width, pair_width)
        return jnp.dot(
            normed[...], w_qkv[:, pl.ds(start, pair_width)], preferred_element_type=jnp.float32
        )

    def project_keys(step, carry):
        group = group_at(step)
        key_pair = product(1, group)
        value_pair = product(2, group)
        for j in range(2):
            lanes = slice(j * LANES, (j + 1) * LANES)
            key = rotate(key_pair[:, lanes], 1.0).astype(kv_send.dtype)
            value = value_pair[:, lanes].astype(kv_send.dtype)
            for c in range(copies):
                rows = slice(c * padded, (c + 1) * padded)
                unit = group * per_group + j * copies + c
                kv_send[unit, 0] = key[rows]
                kv_send[unit, 1] = value[rows]

        def push(inner, carry):
            unit = group * per_group + inner
            for sub in range(subs):

                @pl.when(unit * subs + sub != me)
                def _():
                    key_value_copy(unit, sub).start()

                @pl.when(unit * subs + sub == me)
                def _():
                    kv_recv[me, :, own_rows] = kv_send[unit, :, own_rows]

            return carry

        lax.fori_loop(0, per_group, push, 0)
        return carry

    def project_queries(step, carry):
        group = group_at(step)
        query_pair = product(0, group)
        for j in range(2):
            lanes = slice(j * LANES, (j + 1) * LANES)
            query = rotate(query_pair[:, lanes], HEAD_DIM**-0.5).astype(q_send.dtype)
            for c in range(copies):
                rows = slice(c * padded, (c + 1) * padded)
                q_send[group * per_group + j * copies + c] = query[rows]

        def push(inner, carry):
            unit = group * per_group + inner

            @pl.when(unit * subs + query_sub != me)
            def _():
                query_copy(unit).start()

            @pl.when(unit * subs + query_sub == me)
            def _():
                q_recv[query_slot, own_rows] = q_send[unit, own_rows]

            return carry

        lax.fori_loop(0, per_group, push, 0)
        return carry

    lax.fori_loop(0, GROUPS, project_keys, 0)
    lax.fori_loop(0, GROUPS, project_queries, 0)

    def arrived(block, semaphores, slot, source):
        pltpu.make_async_remote_copy(
            src_ref=block,
            dst_ref=block,
            send_sem=semaphores.at[slot],
            recv_sem=semaphores.at[slot],
            device_id={"seq": source},
            device_id_type=MESH,
        ).wait_recv()

    def wait_keys(source, carry):
        @pl.when(source != me)
        def _():
            arrived(kv_recv.at[source, :, own_rows], kv_recv_sem, source, source)

        return carry

    lax.fori_loop(0, count, wait_keys, 0)

    def returned(slot):
        return pltpu.make_async_remote_copy(
            src_ref=o_send.at[slot, own_rows],
            dst_ref=o_recv.at[my_unit, own_rows],
            send_sem=o_send_sem.at[slot],
            recv_sem=o_recv_sem.at[my_unit],
            device_id={"seq": my_sub * units + slot},
            device_id_type=MESH,
        )

    first_head = lane < HEAD_DIM
    keys_total = count * padded

    def attend(step, carry):
        base = group_at(step * BLOCKS // per_group) * per_group + step * BLOCKS % per_group
        for i in range(BLOCKS):
            source = my_sub * units + base + i

            @pl.when(source != me)
            def _():
                arrived(q_recv.at[base + i, own_rows], q_recv_sem, base + i, source)

        queries = [q_recv[base + i] for i in range(BLOCKS)]
        nothing = jnp.zeros_like(queries[0])
        both = jnp.concatenate(
            [jnp.where(first_head, query, nothing) for query in queries]
            + [jnp.where(first_head, nothing, query) for query in queries],
            axis=0,
        )
        keys = kv_recv[:, 0].reshape(keys_total, LANES)
        values = kv_recv[:, 1].reshape(keys_total, LANES)
        scores = lax.dot_general(
            both, keys, (((1,), (1,)), ((), ())), preferred_element_type=jnp.float32
        )
        scores = scores + bias[0:1, :]
        peak = jnp.max(scores, axis=-1, keepdims=True)
        exponentials = jnp.exp(scores - peak)
        weight_sum = jnp.sum(exponentials, axis=-1, keepdims=True)
        weighted = jnp.dot(
            exponentials.astype(values.dtype), values, preferred_element_type=jnp.float32
        )
        weighted = weighted / weight_sum
        half = BLOCKS * padded
        for i in range(BLOCKS):
            slot = base + i
            rows = slice(i * padded, (i + 1) * padded)
            o_send[slot] = jnp.where(first_head, weighted[:half][rows], weighted[half:][rows]).astype(
                o_send.dtype
            )

            @pl.when(my_sub * units + slot != me)
            def _():
                returned(slot).start()

            @pl.when(my_sub * units + slot == me)
            def _():
                o_recv[my_unit, own_rows] = o_send[slot, own_rows]

        return carry

    lax.fori_loop(0, units // BLOCKS, attend, 0)

    def wait_attended(unit, carry):
        @pl.when(unit * subs + query_sub != me)
        def _():
            arrived(o_recv.at[unit, own_rows], o_recv_sem, unit, unit * subs + query_sub)

        return carry

    lax.fori_loop(0, units, wait_attended, 0)
    for unit in range(units):
        attended[
            pl.ds((unit % copies) * padded, padded), pl.ds((unit // copies) * LANES, LANES)
        ] = o_recv[unit]
    for copy in late:
        copy.wait()

    def merge(block, carry):
        columns = pl.ds(pl.multiple_of(block * pair_width, pair_width), pair_width)
        branch = jnp.dot(attended[...], w_out[:, columns], preferred_element_type=jnp.float32)
        residual[:, columns] = residual[:, columns] + modulation[2:3, columns] * branch
        return carry

    lax.fori_loop(0, width // pair_width, merge, 0)
    normalise(3)
    speed = lax.dot_general(
        normed[...], w_mel[...], (((1,), (1,)), ((), ())), preferred_element_type=jnp.float32
    )
    speed_first = speed[:frame_rows]
    speed_second = speed[padded : padded + frame_rows]
    guided_ref[...] = speed_first + guidance_ref[0] * (speed_first - speed_second)

    def finish(unit, carry):
        @pl.when(unit * subs + query_sub != me)
        def _():
            query_copy(unit).wait_send()

        for sub in range(subs):

            @pl.when(unit * subs + sub != me)
            def _():
                key_value_copy(unit, sub).wait_send()

        @pl.when(my_sub * units + unit != me)
        def _():
            returned(unit).wait_send()

        return carry

    lax.fori_loop(0, units, finish, 0)


def rotary_tables(padded, count, frame_rows):
    half = HEAD_DIM // 2
    inverse = 10000.0 ** (-(np.arange(LANES) % half) / half)
    rows = np.arange(padded)[:, None] * inverse[None, :]
    bases = (np.arange(count) * frame_rows)[:, None] * inverse[None, :]
    row_table = np.stack([np.cos(rows), np.sin(rows)]).astype(np.float32)
    base_table = np.stack([np.cos(bases), np.sin(bases)], axis=1).astype(np.float32)
    return row_table, base_table


def per_device(
    hidden, latent, lengths, step_index, guidance, modulation, conv_kernel, w_qkv, w_out, w_mel
):
    copies, frame_rows, width = hidden.shape
    taps = conv_kernel.shape[0]
    mel = w_mel.shape[1]
    attention_width = w_out.shape[0]
    count = lax.axis_size("seq")
    units = copies * HEADS * HEAD_DIM // LANES
    subs = count // units
    assert subs * units == count
    padded = -(-frame_rows // 16) * 16
    reach = -(-(taps // 2 + 1) // 8) * 8
    row_table, base_table = rotary_tables(padded, count, frame_rows)
    bf16 = jnp.bfloat16
    f32 = jnp.float32
    dma = pltpu.SemaphoreType.DMA
    anywhere = pl.BlockSpec(memory_space=pl.ANY)
    scalar = pl.BlockSpec(memory_space=pltpu.SMEM)
    guided = pl.pallas_call(
        functools.partial(kernel, count, subs, frame_rows, taps),
        out_shape=jax.ShapeDtypeStruct((frame_rows, mel), f32),
        in_specs=[scalar, scalar] + [anywhere] * 8,
        out_specs=pl.BlockSpec(memory_space=pltpu.VMEM),
        scratch_shapes=[
            pltpu.VMEM((copies, padded, width), bf16),
            pltpu.VMEM((2, copies, reach, width), bf16),
            pltpu.VMEM(modulation.shape, f32),
            pltpu.VMEM(conv_kernel.shape, f32),
            pltpu.VMEM(w_qkv.shape, bf16),
            pltpu.VMEM(w_out.shape, bf16),
            pltpu.VMEM((mel, width), bf16),
            pltpu.VMEM(row_table.shape, f32),
            pltpu.VMEM(base_table.shape[1:], f32),
            pltpu.VMEM((2, copies * padded, LANES), f32),
            pltpu.VMEM((copies * padded, width), f32),
            pltpu.VMEM((copies * padded, width), bf16),
            pltpu.VMEM((units, padded, LANES), bf16),
            pltpu.VMEM((units, 2, padded, LANES), bf16),
            pltpu.VMEM((units, padded, LANES), bf16),
            pltpu.VMEM((count, 2, padded, LANES), bf16),
            pltpu.VMEM((units, padded, LANES), bf16),
            pltpu.VMEM((units, padded, LANES), bf16),
            pltpu.VMEM((copies * padded, attention_width), bf16),
            pltpu.VMEM((8, count * padded), f32),
            dma((7,)),
            dma((6,)),
            dma((2,)),
            dma((2,)),
            dma((units,)),
            dma((units,)),
            dma((count,)),
            dma((count,)),
            dma((units,)),
            dma((units,)),
        ],
        compiler_params=pltpu.CompilerParams(
            collective_id=0, has_side_effects=True, vmem_limit_bytes=56 * 1024 * 1024
        ),
    )(
        lengths,
        guidance,
        hidden,
        modulation,
        conv_kernel,
        w_qkv,
        w_out,
        w_mel.T,
        jnp.asarray(row_table),
        jnp.asarray(base_table),
    )
    positions = lax.axis_index("seq") * frame_rows + jnp.arange(frame_rows, dtype=jnp.int32)
    velocity = jnp.where((positions < lengths[0])[:, None], guided, 0.0)
    progress = step_index[0].astype(f32) / STEPS
    time_now = 1.0 - jnp.cos(0.5 * jnp.pi * progress)
    estimate = latent + (1.0 - time_now) * velocity
    return (velocity, estimate)


def solution(mesh):
    return jax.shard_map(
        per_device,
        mesh=mesh,
        in_specs=(
            P(None, ("clip", "seq"), None),
            P(("clip", "seq"), None),
            P("clip"),
            P(),
            P(),
            P(),
            P(),
            P(),
            P(),
            P(),
        ),
        out_specs=(P(("clip", "seq"), None), P(("clip", "seq"), None)),
        check_vma=False,
    )
```

profile of v0, /device:TPU:0, one launch (start us, length us, event | category | flops | bytes accessed | tf_op | source)
XLA Modules:
  0.0 47.3 jit_solution(13092949193901162081)
XLA Ops:
  0.6 0.0 copy-start
  2.7 43.2 %shard_map.131 = f32[56,100]{1,0:T(8,128)} custom-call(s32[1]{0:T(128)} %copy.14.length_ref, f32[1]{0:T(128)S(6)} %copy.16.guidance_ref, bf16[2,56,1536]{2,1,0:T(8,128)(2,1)} %hidden_hbm.1, f32[5,1536]{1,0:T(8,128)} %modulation_hbm.1, f32[31,1536]{1,0:T(8,128)} %conv_hbm.1, bf16[1536,3072]{1,0:T(8,128)(2,1)} %qkv_hbm.1, bf16[1024,1536]{1,0:T(8,128)(2,1)} %out_hbm.1, ...), custom_call_target="tpu_custom_call" | custom-call | tf_op jit(solution)/shard_map/pallas_call | solution.py:526
  45.9 0.0 copy-done
  45.9 1.4 %multiply_add_fusion = (f32[56,100]{1,0:T(8,128)}, f32[56,100]{1,0:T(8,128)}) fusion(f32[56,100]{1,0:T(8,128)S(1)} %copy-done, f32[]{:T(128)} %bitcast.2, f32[56,100]{1,0:T(8,128)} %shard_map.131, pred[56]{0:T(512)(128)(4,1)S(1)} %add_compare_fusion), kind=kLoop, calls=%fused_computation | loop fusion | flops 16800 | bytes 89660 | tf_op jit(solution)/shard_map/add | solution.py:582
  (1 shorter events, 0.0 us)
Async XLA Ops:
  0.6 45.2 %copy-start = (f32[56,100]{1,0:T(8,128)S(1)}, f32[56,100]{1,0:T(8,128)}, u32[]{:S(2)}) copy-start(f32[56,100]{1,0:T(8,128)} %param.13) | copy-start | bytes 67204
where the time goes:
time: 47.6 us; the launch traced here: 47.3 us
  Pallas kernels  43.2 us (91%)
  between operations  2.69 us (6%)
  other arithmetic  1.45 us (3%)
    pallas_call x1, Pallas kernels, per_device(): pl.pallas_call(functools.partial(kernel, count, subs, frame_rows, taps),...  43.2 us
    add x1, other arithmetic, per_device(): estimate = latent + (1.0 - time_now) * velocity  1.45 us

commit v1 on v0

v1 whole, which is shorter than its diff:
```python
import functools

import jax
import jax.numpy as jnp
import numpy as np
from jax import lax
from jax.experimental import pallas as pl
from jax.experimental.pallas import tpu as pltpu
from jax.sharding import PartitionSpec as P

HEADS = 16
HEAD_DIM = 64
STEPS = 32
LANES = 128
EPSILON = 1e-06
NEGATIVE = -1e30
MESH = pl.DeviceIdType.MESH
ROW_BLOCK = 16
GROUPS = 4
BLOCKS = 2
PIECES = 2


def layer_norm(values, shift_row, scale_row):
    mean_value = jnp.mean(values, axis=-1, keepdims=True)
    centered = values - mean_value
    variance = jnp.mean(centered * centered, axis=-1, keepdims=True)
    return centered * lax.rsqrt(variance + EPSILON) * (1.0 + scale_row) + shift_row


def mish(values):
    grown = jnp.exp(jnp.minimum(values, 30.0))
    top = grown * (grown + 2.0)
    return values * (top / (top + 2.0))


def kernel(
    count,
    subs,
    frame_rows,
    taps,
    scalars,
    hidden_hbm,
    latent_hbm,
    modulation_hbm,
    conv_hbm,
    qkv_hbm,
    out_hbm,
    mel_hbm,
    row_table_hbm,
    base_table_hbm,
    velocity_ref,
    estimate_ref,
    hid,
    latent,
    halo,
    modulation,
    conv,
    w_qkv,
    w_out,
    w_mel,
    row_table,
    base_table,
    tables,
    residual,
    normed,
    q_send,
    kv_send,
    q_recv,
    kv_recv,
    o_send,
    o_recv,
    bias,
    local_sem,
    qkv_sem,
    halo_send_sem,
    halo_recv_sem,
    q_send_sem,
    q_recv_sem,
    kv_send_sem,
    kv_recv_sem,
    o_send_sem,
    o_recv_sem,
):
    copies = hid.shape[0]
    padded = hid.shape[1]
    reach = halo.shape[2]
    width = hid.shape[2]
    units = q_send.shape[0]
    per_group = units // GROUPS
    attention_width = w_out.shape[0]
    me = lax.axis_index("seq")
    own_rows = pl.ds(0, frame_rows)

    pulls = [
        (hidden_hbm, hid.at[:, pl.ds(0, frame_rows), :]),
        (conv_hbm, conv),
        (modulation_hbm, modulation),
        (row_table_hbm, row_table),
        (base_table_hbm.at[me], base_table),
        (latent_hbm, latent),
    ]
    local = [
        pltpu.make_async_copy(source, target, local_sem.at[i])
        for i, (source, target) in enumerate(pulls)
    ]
    for copy in local:
        copy.start()

    barrier = pltpu.get_barrier_semaphore()

    def greet(step, carry):
        pl.semaphore_signal(
            barrier, inc=1, device_id={"seq": (me + step) % count}, device_id_type=MESH
        )
        return carry

    lax.fori_loop(1, count, greet, 0)
    chunks = qkv_sem.shape[0]
    depth = width // chunks
    weights = [
        pltpu.make_async_copy(
            qkv_hbm.at[pl.ds(i * depth, depth)], w_qkv.at[pl.ds(i * depth, depth)], qkv_sem.at[i]
        )
        for i in range(chunks)
    ]
    late = [
        pltpu.make_async_copy(out_hbm, w_out, local_sem.at[len(pulls)]),
        pltpu.make_async_copy(mel_hbm, w_mel, local_sem.at[len(pulls) + 1]),
    ]
    for copy in weights + late:
        copy.start()
    hid[:, pl.ds(frame_rows, padded - frame_rows), :] = jnp.zeros(
        (copies, padded - frame_rows, width), hid.dtype
    )
    spare = pl.ds(frame_rows, padded - frame_rows)
    for buffer in (q_recv, o_recv):
        buffer[:, spare, :] = jnp.zeros((units, padded - frame_rows, LANES), buffer.dtype)
    kv_recv[:, :, spare, :] = jnp.zeros((count, 2, padded - frame_rows, LANES), kv_recv.dtype)

    pl.semaphore_wait(barrier, count - 1)
    piece_width = width // PIECES

    def halo_copies(c, piece):
        columns = pl.ds(piece * piece_width, piece_width)
        slot = c * PIECES + piece
        to_right = pltpu.make_async_remote_copy(
            src_ref=hidden_hbm.at[c, pl.ds(frame_rows - reach, reach), columns],
            dst_ref=halo.at[0, c, :, columns],
            send_sem=halo_send_sem.at[0, slot],
            recv_sem=halo_recv_sem.at[0, slot],
            device_id={"seq": (me + 1) % count},
            device_id_type=MESH,
        )
        to_left = pltpu.make_async_remote_copy(
            src_ref=hidden_hbm.at[c, pl.ds(0, reach), columns],
            dst_ref=halo.at[1, c, :, columns],
            send_sem=halo_send_sem.at[1, slot],
            recv_sem=halo_recv_sem.at[1, slot],
            device_id={"seq": (me + count - 1) % count},
            device_id_type=MESH,
        )
        return to_right, to_left

    halos = [halo_copies(c, piece) for c in range(copies) for piece in range(PIECES)]

    @pl.when(me < count - 1)
    def _():
        for to_right, _ in halos:
            to_right.start()

    @pl.when(me > 0)
    def _():
        for _, to_left in halos:
            to_left.start()

    @pl.when(me == 0)
    def _():
        halo[0] = jnp.zeros(halo.shape[1:], halo.dtype)

    @pl.when(me == count - 1)
    def _():
        halo[1] = jnp.zeros(halo.shape[1:], halo.dtype)

    for copy in local:
        copy.wait()
    length = scalars[0:1, :].astype(jnp.int32)

    base_cos = base_table[0:1, :]
    base_sin = base_table[1:2, :]
    row_cos = row_table[0]
    row_sin = row_table[1]
    lane = lax.broadcasted_iota(jnp.int32, (padded, LANES), 1)
    lower = lane % HEAD_DIM < HEAD_DIM // 2
    tables[0] = row_cos * base_cos - row_sin * base_sin
    sine = row_sin * base_cos + row_cos * base_sin
    tables[1] = jnp.where(lower, -sine, sine)
    key_index = lax.broadcasted_iota(jnp.int32, bias.shape, 1)
    key_row = key_index % padded
    key_position = (key_index // padded) * frame_rows + key_row
    key_live = (key_row < frame_rows) & (key_position < length[:, 0:1])
    bias[...] = jnp.where(key_live, 0.0, NEGATIVE)

    window = frame_rows + 2 * reach
    position = (
        me * frame_rows - reach + lax.broadcasted_iota(jnp.int32, (window, LANES), 0)
    )
    is_live = (position >= 0) & (position < length)
    lead = reach - taps // 2

    def convolve(c):
        def one(block, carry):
            columns = pl.ds(pl.multiple_of(block * LANES, LANES), LANES)
            own = hid[c, :, columns].astype(jnp.float32)
            cells = jnp.concatenate(
                [
                    halo[0, c, :, columns].astype(jnp.float32),
                    own[:frame_rows],
                    halo[1, c, :, columns].astype(jnp.float32),
                ],
                axis=0,
            )
            cells = jnp.where(is_live, cells, 0.0)
            total = jnp.zeros((padded, LANES), jnp.float32)
            for shift in range(8):
                part = None
                for first in range(0, reach * 2, 8):
                    tap = first + shift - lead
                    if 0 <= tap < taps:
                        term = cells[first : first + padded] * conv[pl.ds(tap, 1), columns]
                        part = term if part is None else part + term
                if part is not None:
                    total = total + (pltpu.roll(part, padded - shift, 0) if shift else part)
            residual[pl.ds(c * padded, padded), columns] = own + mish(total)
            return carry

        return one

    def convolve_copy(c):
        blocks = piece_width // LANES
        for piece in range(PIECES):
            to_right, to_left = halos[c * PIECES + piece]

            @pl.when(me < count - 1)
            def _():
                to_left.wait_recv()

            @pl.when(me > 0)
            def _():
                to_right.wait_recv()

            lax.fori_loop(piece * blocks, (piece + 1) * blocks, convolve(c), 0)

    def normalise(first, start, stop):
        for row in range(start, stop, ROW_BLOCK):
            rows = pl.ds(row, ROW_BLOCK)
            normed[rows, :] = layer_norm(
                residual[rows, :], modulation[first : first + 1, :], modulation[first + 1 : first + 2, :]
            ).astype(normed.dtype)

    my_group = me * GROUPS // count
    my_high = my_group // 2
    my_low = my_group % 2

    def group_at(step):
        return ((my_high + (3 - step) // 2) % 2) * 2 + (my_low + (step + 1) // 2) % 2

    my_unit = me // subs
    my_sub = me % subs
    query_sub = me // units
    query_slot = me % units

    def query_copy(unit):
        return pltpu.make_async_remote_copy(
            src_ref=q_send.at[unit, own_rows],
            dst_ref=q_recv.at[query_slot, own_rows],
            send_sem=q_send_sem.at[unit],
            recv_sem=q_recv_sem.at[query_slot],
            device_id={"seq": unit * subs + query_sub},
            device_id_type=MESH,
        )

    def key_value_copy(unit, sub):
        return pltpu.make_async_remote_copy(
            src_ref=kv_send.at[unit, :, own_rows],
            dst_ref=kv_recv.at[me, :, own_rows],
            send_sem=kv_send_sem.at[unit * subs + sub],
            recv_sem=kv_recv_sem.at[me],
            device_id={"seq": unit * subs + sub},
            device_id_type=MESH,
        )

    pair_width = 2 * LANES

    def rotate(tile, factor):
        half = HEAD_DIM // 2
        other = jnp.where(lower, pltpu.roll(tile, LANES - half, 1), pltpu.roll(tile, half, 1))
        return (tile * tables[0] + other * tables[1]) * factor

    def product(part, group, start, stop):
        first = pl.multiple_of(part * attention_width + group * pair_width, pair_width)
        return jnp.dot(
            normed[start:stop, :],
            w_qkv[:, pl.ds(first, pair_width)],
            preferred_element_type=jnp.float32,
        )

    def project_keys(c):
        def one(step, carry):
            group = group_at(step)
            key_pair = product(1, group, c * padded, (c + 1) * padded)
            value_pair = product(2, group, c * padded, (c + 1) * padded)
            for j in range(2):
                lanes = slice(j * LANES, (j + 1) * LANES)
                unit = group * per_group + j * copies + c
                kv_send[unit, 0] = rotate(key_pair[:, lanes], 1.0).astype(kv_send.dtype)
                kv_send[unit, 1] = value_pair[:, lanes].astype(kv_send.dtype)
            for j in range(2):
                unit = group * per_group + j * copies + c
                for sub in range(subs):

                    @pl.when(unit * subs + sub != me)
                    def _():
                        key_value_copy(unit, sub).start()

                    @pl.when(unit * subs + sub == me)
                    def _():
                        kv_recv[me, :, own_rows] = kv_send[unit, :, own_rows]

            return carry

        return one

    def project_queries(step, carry):
        group = group_at(step)
        query_pair = product(0, group, 0, copies * padded)
        for j in range(2):
            lanes = slice(j * LANES, (j + 1) * LANES)
            for c in range(copies):
                q_send[group * per_group + j * copies + c] = rotate(
                    query_pair[c * padded : (c + 1) * padded, lanes], HEAD_DIM**-0.5
                ).astype(q_send.dtype)

        def push(inner, carry):
            unit = group * per_group + inner

            @pl.when(unit * subs + query_sub != me)
            def _():
                query_copy(unit).start()

            @pl.when(unit * subs + query_sub == me)
            def _():
                q_recv[query_slot, own_rows] = q_send[unit, own_rows]

            return carry

        lax.fori_loop(0, per_group, push, 0)
        return carry

    for c in range(copies):
        convolve_copy(c)
        normalise(0, c * padded, (c + 1) * padded)
        if c == 0:
            for copy in weights:
                copy.wait()
        lax.fori_loop(0, GROUPS, project_keys(c), 0)
    lax.fori_loop(0, GROUPS, project_queries, 0)

    def arrived(block, semaphores, slot, source):
        pltpu.make_async_remote_copy(
            src_ref=block,
            dst_ref=block,
            send_sem=semaphores.at[slot],
            recv_sem=semaphores.at[slot],
            device_id={"seq": source},
            device_id_type=MESH,
        ).wait_recv()

    def wait_keys(source, carry):
        @pl.when(source != me)
        def _():
            arrived(kv_recv.at[source, :, own_rows], kv_recv_sem, source, source)

        return carry

    lax.fori_loop(0, count, wait_keys, 0)

    def returned(slot):
        return pltpu.make_async_remote_copy(
            src_ref=o_send.at[slot, own_rows],
            dst_ref=o_recv.at[my_unit, own_rows],
            send_sem=o_send_sem.at[slot],
            recv_sem=o_recv_sem.at[my_unit],
            device_id={"seq": my_sub * units + slot},
            device_id_type=MESH,
        )

    first_head = lane < HEAD_DIM
    keys_total = count * padded
    rounds = per_group // BLOCKS

    def attend(step, carry):
        pair = step // (2 * rounds)
        inner = step % (2 * rounds)
        group = ((my_high + inner % 2) % 2) * 2 + (my_low + pair) % 2
        base = group * per_group + (inner // 2) * BLOCKS
        for i in range(BLOCKS):
            source = my_sub * units + base + i

            @pl.when(source != me)
            def _():
                arrived(q_recv.at[base + i, own_rows], q_recv_sem, base + i, source)

        queries = [q_recv[base + i] for i in range(BLOCKS)]
        nothing = jnp.zeros_like(queries[0])
        both = jnp.concatenate(
            [jnp.where(first_head, query, nothing) for query in queries]
            + [jnp.where(first_head, nothing, query) for query in queries],
            axis=0,
        )
        keys = kv_recv[:, 0].reshape(keys_total, LANES)
        values = kv_recv[:, 1].reshape(keys_total, LANES)
        scores = lax.dot_general(
            both, keys, (((1,), (1,)), ((), ())), preferred_element_type=jnp.float32
        )
        scores = scores + bias[0:1, :]
        peak = jnp.max(scores, axis=-1, keepdims=True)
        exponentials = jnp.exp(scores - peak)
        weight_sum = jnp.sum(exponentials, axis=-1, keepdims=True)
        weighted = jnp.dot(
            exponentials.astype(values.dtype), values, preferred_element_type=jnp.float32
        )
        weighted = weighted / weight_sum
        half = BLOCKS * padded
        for i in range(BLOCKS):
            slot = base + i
            rows = slice(i * padded, (i + 1) * padded)
            o_send[slot] = jnp.where(first_head, weighted[:half][rows], weighted[half:][rows]).astype(
                o_send.dtype
            )

            @pl.when(my_sub * units + slot != me)
            def _():
                returned(slot).start()

            @pl.when(my_sub * units + slot == me)
            def _():
                o_recv[my_unit, own_rows] = o_send[slot, own_rows]

        return carry

    lax.fori_loop(0, units // BLOCKS, attend, 0)

    def sent(unit, carry):
        @pl.when(unit * subs + query_sub != me)
        def _():
            query_copy(unit).wait_send()

        for sub in range(subs):

            @pl.when(unit * subs + sub != me)
            def _():
                key_value_copy(unit, sub).wait_send()

        return carry

    lax.fori_loop(0, units, sent, 0)

    @pl.when(me < count - 1)
    def _():
        for to_right, _ in halos:
            to_right.wait_send()

    @pl.when(me > 0)
    def _():
        for _, to_left in halos:
            to_left.wait_send()

    for copy in late:
        copy.wait()

    def merge(step, carry):
        group = ((my_high + step % 2) % 2) * 2 + (my_low + step // 2) % 2
        for inner in range(per_group):
            unit = group * per_group + inner

            @pl.when(unit * subs + query_sub != me)
            def _():
                arrived(o_recv.at[unit, own_rows], o_recv_sem, unit, unit * subs + query_sub)

        attended = jnp.concatenate(
            [
                jnp.concatenate(
                    [o_recv[group * per_group + j * copies + c] for j in range(2)], axis=1
                )
                for c in range(copies)
            ],
            axis=0,
        )
        depth_rows = pl.ds(pl.multiple_of(group * pair_width, pair_width), pair_width)
        for first in range(0, width, pair_width):
            columns = slice(first, first + pair_width)
            branch = jnp.dot(attended, w_out[depth_rows, columns], preferred_element_type=jnp.float32)
            residual[:, columns] = residual[:, columns] + modulation[2:3, columns] * branch
        return carry

    lax.fori_loop(0, GROUPS, merge, 0)
    normalise(3, 0, copies * padded)
    speed = lax.dot_general(
        normed[...], w_mel[...], (((1,), (1,)), ((), ())), preferred_element_type=jnp.float32
    )
    speed_first = speed[:frame_rows]
    speed_second = speed[padded : padded + frame_rows]
    mel = speed.shape[1]
    guided = speed_first + scalars[2:3, :mel] * (speed_first - speed_second)
    own_position = me * frame_rows + lax.broadcasted_iota(jnp.int32, guided.shape, 0)
    velocity = jnp.where(own_position < length[:, :mel], guided, 0.0)
    progress = scalars[1:2, :mel] / STEPS
    time_now = 1.0 - jnp.cos(0.5 * jnp.pi * progress)
    velocity_ref[...] = velocity
    estimate_ref[...] = latent[...] + (1.0 - time_now) * velocity

    def finish(slot, carry):
        @pl.when(my_sub * units + slot != me)
        def _():
            returned(slot).wait_send()

        return carry

    lax.fori_loop(0, units, finish, 0)


def rotary_tables(padded, count, frame_rows):
    half = HEAD_DIM // 2
    inverse = 10000.0 ** (-(np.arange(LANES) % half) / half)
    rows = np.arange(padded)[:, None] * inverse[None, :]
    bases = (np.arange(count) * frame_rows)[:, None] * inverse[None, :]
    row_table = np.stack([np.cos(rows), np.sin(rows)]).astype(np.float32)
    base_table = np.stack([np.cos(bases), np.sin(bases)], axis=1).astype(np.float32)
    return row_table, base_table


def per_device(
    hidden, latent, lengths, step_index, guidance, modulation, conv_kernel, w_qkv, w_out, w_mel
):
    copies, frame_rows, width = hidden.shape
    taps = conv_kernel.shape[0]
    mel = w_mel.shape[1]
    count = lax.axis_size("seq")
    units = copies * HEADS * HEAD_DIM // LANES
    subs = count // units
    assert subs * units == count
    padded = -(-frame_rows // 16) * 16
    reach = -(-(taps // 2 + 1) // 8) * 8
    row_table, base_table = rotary_tables(padded, count, frame_rows)
    bf16 = jnp.bfloat16
    f32 = jnp.float32
    dma = pltpu.SemaphoreType.DMA
    scalars = jnp.concatenate(
        [
            jnp.broadcast_to(value.astype(f32)[:, None], (1, LANES))
            for value in (lengths, step_index, guidance)
        ]
    )
    return pl.pallas_call(
        functools.partial(kernel, count, subs, frame_rows, taps),
        out_shape=[pltpu.VMEM((frame_rows, mel), f32)] * 2,
        in_specs=[pl.BlockSpec(memory_space=pltpu.VMEM)] + [pl.BlockSpec(memory_space=pl.ANY)] * 9,
        out_specs=[pl.BlockSpec(memory_space=pltpu.VMEM)] * 2,
        scratch_shapes=[
            pltpu.VMEM((copies, padded, width), bf16),
            pltpu.VMEM((frame_rows, mel), f32),
            pltpu.VMEM((2, copies, reach, width), bf16),
            pltpu.VMEM(modulation.shape, f32),
            pltpu.VMEM(conv_kernel.shape, f32),
            pltpu.VMEM(w_qkv.shape, bf16),
            pltpu.VMEM(w_out.shape, bf16),
            pltpu.VMEM((mel, width), bf16),
            pltpu.VMEM(row_table.shape, f32),
            pltpu.VMEM(base_table.shape[1:], f32),
            pltpu.VMEM((2, padded, LANES), f32),
            pltpu.VMEM((copies * padded, width), f32),
            pltpu.VMEM((copies * padded, width), bf16),
            pltpu.VMEM((units, padded, LANES), bf16),
            pltpu.VMEM((units, 2, padded, LANES), bf16),
            pltpu.VMEM((units, padded, LANES), bf16),
            pltpu.VMEM((count, 2, padded, LANES), bf16),
            pltpu.VMEM((units, padded, LANES), bf16),
            pltpu.VMEM((units, padded, LANES), bf16),
            pltpu.VMEM((8, count * padded), f32),
            dma((8,)),
            dma((6,)),
            dma((2, copies * PIECES)),
            dma((2, copies * PIECES)),
            dma((units,)),
            dma((units,)),
            dma((count,)),
            dma((count,)),
            dma((units,)),
            dma((units,)),
        ],
        compiler_params=pltpu.CompilerParams(
            collective_id=0, has_side_effects=True, vmem_limit_bytes=40 * 1024 * 1024
        ),
    )(
        pltpu.with_memory_space_constraint(scalars, pltpu.VMEM),
        *(
            pltpu.with_memory_space_constraint(operand, pltpu.HBM)
            for operand in (
                hidden,
                latent,
                modulation,
                conv_kernel,
                w_qkv,
                w_out,
                w_mel.T,
                jnp.asarray(row_table),
                jnp.asarray(base_table),
            )
        )
    )


def solution(mesh):
    return jax.shard_map(
        per_device,
        mesh=mesh,
        in_specs=(
            P(None, ("clip", "seq"), None),
            P(("clip", "seq"), None),
            P("clip"),
            P(),
            P(),
            P(),
            P(),
            P(),
            P(),
            P(),
        ),
        out_specs=(P(("clip", "seq"), None), P(("clip", "seq"), None)),
        check_vma=False,
    )
```

time: 47.6 us -> 40 us (0.84)
  Pallas kernels: 43.2 us -> 35.9 us
  other arithmetic: 1.45 us -> 0.08 us
  local copies, waits for them, and re-layouts: 0.01 us -> 1.29 us
    pallas_call x1, Pallas kernels: 43.2 us -> 35.9 us  [per_device(): pl.pallas_call(functools.partial(kernel, count, subs, frame_rows, taps),...]
    add x1 -> x0, other arithmetic: 1.45 us -> none  [per_device(): estimate = latent + (1.0 - time_now) * velocity]
    unnamed x2, local copies, waits for them, and re-layouts: 0.01 us -> 1.22 us
where the time goes in v1:
time: 40 us; the launch traced here: 39.9 us
  Pallas kernels  35.9 us (90%)
  between operations  2.58 us (6%)
  local copies, waits for them, and re-layouts  1.29 us (3%)
    pallas_call x1, Pallas kernels, per_device(): pl.pallas_call(functools.partial(kernel, count, subs, frame_rows, taps),...  35.9 us
    unnamed x2, local copies, waits for them, and re-layouts  1.22 us

profile of v1, /device:TPU:0, one launch (start us, length us, event | category | flops | bytes accessed | tf_op | source)
XLA Modules:
  0.0 39.9 jit_solution(4715304330504941174)
XLA Ops:
  2.6 0.1 maximum_maximum_fusion
  2.6 0.1 broadcast.7.scalars
  2.7 35.9 %shard_map.131 = (f32[56,100]{1,0:T(8,128)S(1)}, f32[56,100]{1,0:T(8,128)S(1)}) custom-call(f32[3,128]{1,0:T(4,128)S(1)} %broadcast.7.scalars, bf16[2,56,1536]{2,1,0:T(8,128)(2,1)} %hidden_hbm.1, f32[56,100]{1,0:T(8,128)} %latent_hbm.1, f32[5,1536]{1,0:T(8,128)} %modulation_hbm.1, f32[31,1536]{1,0:T(8,128)} %conv_hbm.1, bf16[1536,3072]{1,0:T(8,128)(2,1)} %qkv_hbm.1, ...), custom_call_target="tpu_custom_call" | custom-call | tf_op jit(solution)/shard_map/pallas_call | solution.py:565
  38.6 0.6 %copy.16 = f32[56,100]{1,0:T(8,128)} copy(f32[56,100]{1,0:T(8,128)S(1)} %get-tuple-element.2) | data formatting | bytes 44800
  39.3 0.6 %copy.17 = f32[56,100]{1,0:T(8,128)} copy(f32[56,100]{1,0:T(8,128)S(1)} %get-tuple-element.3) | data formatting | bytes 44800

commit v2 on v1

--- a/solution.py
+++ b/solution.py
@@ -81,6 +81,8 @@
     kv_recv_sem,
     o_send_sem,
     o_recv_sem,
+    from_below,
+    from_above,
 ):
     copies = hid.shape[0]
     padded = hid.shape[1]
@@ -109,26 +111,67 @@
 
     barrier = pltpu.get_barrier_semaphore()
 
+    def signal(semaphore, target):
+        pl.semaphore_signal(semaphore, inc=1, device_id={"seq": target}, device_id_type=MESH)
+
+    plane = count // GROUPS
+    my_group = me // plane
+    my_place = me % plane
+    below = my_group > 0
+    above = my_group < GROUPS - 1
+    first_place = my_place == 0
+    last_place = my_place == plane - 1
+
     def greet(step, carry):
-        pl.semaphore_signal(
-            barrier, inc=1, device_id={"seq": (me + step) % count}, device_id_type=MESH
-        )
+        signal(barrier, my_group * plane + (my_place + step) % plane)
         return carry
 
-    lax.fori_loop(1, count, greet, 0)
-    chunks = qkv_sem.shape[0]
-    depth = width // chunks
-    weights = [
-        pltpu.make_async_copy(
-            qkv_hbm.at[pl.ds(i * depth, depth)], w_qkv.at[pl.ds(i * depth, depth)], qkv_sem.at[i]
-        )
-        for i in range(chunks)
-    ]
+    @pl.when(below)
+    def _():
+        signal(barrier, me - plane)
+
+    @pl.when(above)
+    def _():
+        signal(barrier, me + plane)
+
+    @pl.when(below & first_place)
+    def _():
+        signal(barrier, me - 1)
+
+    @pl.when(above & last_place)
+    def _():
+        signal(barrier, me + 1)
+
+    lax.fori_loop(1, plane, greet, 0)
+    my_high = my_group // 2
+    my_low = my_group % 2
+
+    def group_at(step):
+        return ((my_high + (3 - step) // 2) % 2) * 2 + (my_low + (step + 1) // 2) % 2
+
+    pair_width = 2 * LANES
+
+    def weight_columns(part, group):
+        return pl.ds(
+            pl.multiple_of(part * attention_width + group * pair_width, pair_width), pair_width
+        )
+
+    def weight_copy(part, step):
+        columns = weight_columns(part, group_at(step))
+        return pltpu.make_async_copy(
+            qkv_hbm.at[:, columns], w_qkv.at[:, columns], qkv_sem.at[part, step]
+        )
+
     late = [
         pltpu.make_async_copy(out_hbm, w_out, local_sem.at[len(pulls)]),
         pltpu.make_async_copy(mel_hbm, w_mel, local_sem.at[len(pulls) + 1]),
     ]
-    for copy in weights + late:
+    for step in range(GROUPS):
+        weight_copy(1, step).start()
+        weight_copy(2, step).start()
+    for step in range(GROUPS):
+        weight_copy(0, step).start()
+    for copy in late:
         copy.start()
     hid[:, pl.ds(frame_rows, padded - frame_rows), :] = jnp.zeros(
         (copies, padded - frame_rows, width), hid.dtype
@@ -138,7 +181,37 @@
         buffer[:, spare, :] = jnp.zeros((units, padded - frame_rows, LANES), buffer.dtype)
     kv_recv[:, :, spare, :] = jnp.zeros((count, 2, padded - frame_rows, LANES), kv_recv.dtype)
 
-    pl.semaphore_wait(barrier, count - 1)
+    sides = below.astype(jnp.int32) + above.astype(jnp.int32)
+    corners = (below & first_place).astype(jnp.int32) + (above & last_place).astype(jnp.int32)
+    pl.semaphore_wait(barrier, plane - 1 + sides + corners)
+
+    @pl.when(above)
+    def _():
+        signal(from_below.at[0], me + plane)
+
+    @pl.when(below)
+    def _():
+        signal(from_above.at[0], me - plane)
+
+    def relay(hop):
+        @pl.when(my_group >= hop)
+        def _():
+            pl.semaphore_wait(from_below.at[hop - 1], 1)
+
+        @pl.when(GROUPS - 1 - my_group >= hop)
+        def _():
+            pl.semaphore_wait(from_above.at[hop - 1], 1)
+
+        if hop < GROUPS - 1:
+
+            @pl.when((my_group >= hop) & above)
+            def _():
+                signal(from_below.at[hop], me + plane)
+
+            @pl.when((GROUPS - 1 - my_group >= hop) & below)
+            def _():
+                signal(from_above.at[hop], me - plane)
+
     piece_width = width // PIECES
 
     def halo_copies(c, piece):
@@ -182,6 +255,7 @@
     def _():
         halo[1] = jnp.zeros(halo.shape[1:], halo.dtype)
 
+    relay(1)
     for copy in local:
         copy.wait()
     length = scalars[0:1, :].astype(jnp.int32)
@@ -201,42 +275,83 @@
     key_live = (key_row < frame_rows) & (key_position < length[:, 0:1])
     bias[...] = jnp.where(key_live, 0.0, NEGATIVE)
 
-    window = frame_rows + 2 * reach
-    position = (
-        me * frame_rows - reach + lax.broadcasted_iota(jnp.int32, (window, LANES), 0)
-    )
-    is_live = (position >= 0) & (position < length)
+    own_position = me * frame_rows + lax.broadcasted_iota(jnp.int32, (frame_rows, LANES), 0)
+    own_live = own_position < length
+    row16 = lax.broadcasted_iota(jnp.int32, (reach, LANES), 0)
+    right_live = (me + 1) * frame_rows + row16 < length
+    left_live = me * frame_rows - reach + row16 < length
     lead = reach - taps // 2
-
-    def convolve(c):
+    spare_rows = padded - frame_rows
+    tail = reach + spare_rows
+
+    def shifted(part, shift):
+        return pltpu.roll(part, part.shape[0] - shift, 0) if shift else part
+
+    def gather(groups, shift, columns, pieces):
+        part = None
+        for first in groups:
+            tap = first + shift - lead
+            if 0 <= tap < taps:
+                term = pieces(first) * conv[pl.ds(tap, 1), columns]
+                part = term if part is None else part + term
+        return part
+
+    def convolve_own(c):
         def one(block, carry):
             columns = pl.ds(pl.multiple_of(block * LANES, LANES), LANES)
+            own = jnp.where(own_live, hid[c, :frame_rows, columns].astype(jnp.float32), 0.0)
+            blank = jnp.zeros((reach, LANES), jnp.float32)
+            cells = jnp.concatenate([blank, own, blank], axis=0)
+            total = None
+            for shift in range(8):
+                part = gather(
+                    range(0, reach * 2, 8), shift, columns, lambda first: cells[first : first + padded]
+                )
+                part = shifted(part, shift)
+                total = part if total is None else total + part
+            residual[pl.ds(c * padded, padded), columns] = total
+            return carry
+
+        lax.fori_loop(0, width // LANES, one, 0)
+
+    def convolve_edges(c):
+        def one(block, carry):
+            columns = pl.ds(pl.multiple_of(block * LANES, LANES), LANES)
+            left = jnp.where(left_live, halo[0, c, :, columns].astype(jnp.float32), 0.0)
+            right = jnp.where(right_live, halo[1, c, :, columns].astype(jnp.float32), 0.0)
+            blank = jnp.zeros((reach, LANES), jnp.float32)
+            left_cells = jnp.concatenate([left, blank], axis=0)
+            right_cells = jnp.concatenate([blank, right], axis=0)
+            left_total = None
+            right_total = None
+            for shift in range(8):
+                part = gather(
+                    range(0, reach, 8), shift, columns, lambda first: left_cells[first : first + reach]
+                )
+                if part is not None:
+                    part = shifted(jnp.where(row16 < shift, 0.0, part) if shift else part, shift)
+                    left_total = part if left_total is None else left_total + part
+                part = gather(
+                    range(reach, reach * 2, 8),
+                    shift,
+                    columns,
+                    lambda first: right_cells[first - reach : first - reach + tail],
+                )
+                if part is not None:
+                    part = shifted(part, shift)
+                    right_total = part if right_total is None else right_total + part
             own = hid[c, :, columns].astype(jnp.float32)
-            cells = jnp.concatenate(
-                [
-                    halo[0, c, :, columns].astype(jnp.float32),
-                    own[:frame_rows],
-                    halo[1, c, :, columns].astype(jnp.float32),
-                ],
-                axis=0,
-            )
-            cells = jnp.where(is_live, cells, 0.0)
-            total = jnp.zeros((padded, LANES), jnp.float32)
-            for shift in range(8):
-                part = None
-                for first in range(0, reach * 2, 8):
-                    tap = first + shift - lead
-                    if 0 <= tap < taps:
-                        term = cells[first : first + padded] * conv[pl.ds(tap, 1), columns]
-                        part = term if part is None else part + term
-                if part is not None:
-                    total = total + (pltpu.roll(part, padded - shift, 0) if shift else part)
-            residual[pl.ds(c * padded, padded), columns] = own + mish(total)
+            base = c * padded
+            for first, stop in ((0, reach), (reach, padded - tail), (padded - tail, padded)):
+                rows = pl.ds(base + first, stop - first)
+                total = residual[rows, columns]
+                if first == 0:
+                    total = total + left_total
+                if stop == padded:
+                    total = total + right_total
+                residual[rows, columns] = own[first:stop] + mish(total)
             return carry
 
-        return one
-
-    def convolve_copy(c):
         blocks = piece_width // LANES
         for piece in range(PIECES):
             to_right, to_left = halos[c * PIECES + piece]
@@ -249,7 +364,7 @@
             def _():
                 to_right.wait_recv()
 
-            lax.fori_loop(piece * blocks, (piece + 1) * blocks, convolve(c), 0)
+            lax.fori_loop(piece * blocks, (piece + 1) * blocks, one, 0)
 
     def normalise(first, start, stop):
         for row in range(start, stop, ROW_BLOCK):
@@ -257,13 +372,6 @@
             normed[rows, :] = layer_norm(
                 residual[rows, :], modulation[first : first + 1, :], modulation[first + 1 : first + 2, :]
             ).astype(normed.dtype)
-
-    my_group = me * GROUPS // count
-    my_high = my_group // 2
-    my_low = my_group % 2
-
-    def group_at(step):
-        return ((my_high + (3 - step) // 2) % 2) * 2 + (my_low + (step + 1) // 2) % 2
 
     my_unit = me // subs
     my_sub = me % subs
@@ -290,24 +398,24 @@
             device_id_type=MESH,
         )
 
-    pair_width = 2 * LANES
-
     def rotate(tile, factor):
         half = HEAD_DIM // 2
         other = jnp.where(lower, pltpu.roll(tile, LANES - half, 1), pltpu.roll(tile, half, 1))
         return (tile * tables[0] + other * tables[1]) * factor
 
     def product(part, group, start, stop):
-        first = pl.multiple_of(part * attention_width + group * pair_width, pair_width)
         return jnp.dot(
             normed[start:stop, :],
-            w_qkv[:, pl.ds(first, pair_width)],
+            w_qkv[:, weight_columns(part, group)],
             preferred_element_type=jnp.float32,
         )
 
     def project_keys(c):
         def one(step, carry):
             group = group_at(step)
+            if c == 0:
+                weight_copy(1, step).wait()
+                weight_copy(2, step).wait()
             key_pair = product(1, group, c * padded, (c + 1) * padded)
             value_pair = product(2, group, c * padded, (c + 1) * padded)
             for j in range(2):
@@ -333,6 +441,7 @@
 
     def project_queries(step, carry):
         group = group_at(step)
+        weight_copy(0, step).wait()
         query_pair = product(0, group, 0, copies * padded)
         for j in range(2):
             lanes = slice(j * LANES, (j + 1) * LANES)
@@ -357,12 +466,16 @@
         lax.fori_loop(0, per_group, push, 0)
         return carry
 
+    convolve_own(0)
+    for hop in range(2, GROUPS - 1):
+        relay(hop)
     for c in range(copies):
-        convolve_copy(c)
+        if c:
+            convolve_own(c)
+        convolve_edges(c)
         normalise(0, c * padded, (c + 1) * padded)
         if c == 0:
-            for copy in weights:
-                copy.wait()
+            relay(GROUPS - 1)
         lax.fori_loop(0, GROUPS, project_keys(c), 0)
     lax.fori_loop(0, GROUPS, project_queries, 0)
 
@@ -513,8 +626,8 @@
     speed_second = speed[padded : padded + frame_rows]
     mel = speed.shape[1]
     guided = speed_first + scalars[2:3, :mel] * (speed_first - speed_second)
-    own_position = me * frame_rows + lax.broadcasted_iota(jnp.int32, guided.shape, 0)
-    velocity = jnp.where(own_position < length[:, :mel], guided, 0.0)
+    row_position = me * frame_rows + lax.broadcasted_iota(jnp.int32, guided.shape, 0)
+    velocity = jnp.where(row_position < length[:, :mel], guided, 0.0)
     progress = scalars[1:2, :mel] / STEPS
     time_now = 1.0 - jnp.cos(0.5 * jnp.pi * progress)
     velocity_ref[...] = velocity
@@ -589,7 +702,7 @@
             pltpu.VMEM((units, padded, LANES), bf16),
             pltpu.VMEM((8, count * padded), f32),
             dma((8,)),
-            dma((6,)),
+            dma((3, GROUPS)),
             dma((2, copies * PIECES)),
             dma((2, copies * PIECES)),
             dma((units,)),
@@ -598,6 +711,8 @@
             dma((count,)),
             dma((units,)),
             dma((units,)),
+            pltpu.SemaphoreType.REGULAR((GROUPS - 1,)),
+            pltpu.SemaphoreType.REGULAR((GROUPS - 1,)),
         ],
         compiler_params=pltpu.CompilerParams(
             collective_id=0, has_side_effects=True, vmem_limit_bytes=40 * 1024 * 1024

time: 40 us -> 38.2 us (0.955)
  Pallas kernels: 35.9 us -> 34.1 us
    pallas_call x1, Pallas kernels: 35.9 us -> 34.1 us  [per_device(): pl.pallas_call(functools.partial(kernel, count, subs, frame_rows, taps),...]
where the time goes in v2:
time: 38.2 us; the launch traced here: 38 us
  Pallas kernels  34.1 us (89%)
  between operations  2.58 us (7%)
  local copies, waits for them, and re-layouts  1.29 us (3%)
    pallas_call x1, Pallas kernels, per_device(): pl.pallas_call(functools.partial(kernel, count, subs, frame_rows, taps),...  34.1 us
    unnamed x2, local copies, waits for them, and re-layouts  1.22 us

profile of v2, /device:TPU:0, one launch (start us, length us, event | category | flops | bytes accessed | tf_op | source)
XLA Modules:
  0.0 38.0 jit_solution(15579957593850078858)
XLA Ops:
  2.6 0.1 maximum_maximum_fusion
  2.6 0.1 broadcast.7.scalars
  2.7 34.1 %shard_map.131 = (f32[56,100]{1,0:T(8,128)S(1)}, f32[56,100]{1,0:T(8,128)S(1)}) custom-call(f32[3,128]{1,0:T(4,128)S(1)} %broadcast.7.scalars, bf16[2,56,1536]{2,1,0:T(8,128)(2,1)} %hidden_hbm.1, f32[56,100]{1,0:T(8,128)} %latent_hbm.1, f32[5,1536]{1,0:T(8,128)} %modulation_hbm.1, f32[31,1536]{1,0:T(8,128)} %conv_hbm.1, bf16[1536,3072]{1,0:T(8,128)(2,1)} %qkv_hbm.1, ...), custom_call_target="tpu_custom_call" | custom-call | tf_op jit(solution)/shard_map/pallas_call | solution.py:678
  36.8 0.6 %copy.16 = f32[56,100]{1,0:T(8,128)} copy(f32[56,100]{1,0:T(8,128)S(1)} %get-tuple-element.2) | data formatting | bytes 44800
  37.4 0.6 %copy.17 = f32[56,100]{1,0:T(8,128)} copy(f32[56,100]{1,0:T(8,128)S(1)} %get-tuple-element.3) | data formatting | bytes 44800
